TPU v7x, 16 devices: a 4x2x1 block of a 4x4x8 slice. The times are simulated.
16 devices in a mesh: dp: 2 (over y, z), tp: 8 (over x, core).
Axes of the slice: x: 4, y: 2, z: 1, core: 2. Of those that a mesh axis runs over, the one named last changes fastest.
The devices are a block of a 4x4x8 slice.
Arguments:
- x_steps: bfloat16 [16, 128, 4096], P(None, 'dp'), parts along dimension 1
- cur_len: int32 [128], P('dp'), parts along dimension 0
- k_cache: bfloat16 [2, 128, 64, 16, 256], P(None, 'dp', None, 'tp'), parts along dimension 1
- v_cache: bfloat16 [2, 128, 64, 16, 256], P(None, 'dp', None, 'tp'), parts along dimension 1
- ln_gain: bfloat16 [2, 4096], replicated
- ln_bias: bfloat16 [2, 4096], replicated
- w_q: bfloat16 [2, 4096, 4096], P(None, None, 'tp')
- w_k: bfloat16 [2, 4096, 4096], P(None, None, 'tp')
- w_v: bfloat16 [2, 4096, 4096], P(None, None, 'tp')
- w_o: bfloat16 [2, 4096, 4096], P(None, 'tp')
- w_in: bfloat16 [2, 4096, 16384], P(None, None, 'tp')
- b_in: bfloat16 [2, 16384], P(None, 'tp')
- w_out: bfloat16 [2, 16384, 4096], P(None, 'tp')
- b_out: bfloat16 [2, 4096], replicated
Outputs:
- output 1: bfloat16 [16, 128, 4096], P(None, 'dp'), parts along dimension 1
- output 2: bfloat16 [2, 128, 64, 16, 256], P(None, 'dp', None, 'tp'), parts along dimension 1
- output 3: bfloat16 [2, 128, 64, 16, 256], P(None, 'dp', None, 'tp'), parts along dimension 1
There are 2 independent parts. A program takes and returns all parts, laid end to end along the dimension named above; an argument that names none is the same for every part.
All inputs are finite; a program needn't handle non-finite values.
Results may differ from a plain program's by a relative error of at most 0.0170477.
Values are sent between devices in bfloat16 or wider.
A program may use at most 768 MiB of HBM per device.

v0:
```python
import jax
import jax.numpy as jnp
from jax import lax
from jax.sharding import PartitionSpec as P

ROT_DIM = 64
LN_EPS = 1e-5


def layer_norm(hidden, gain, bias):
    hid_f32 = hidden.astype(jnp.float32)
    row_mean = jnp.mean(hid_f32, axis=-1, keepdims=True)
    centered = hid_f32 - row_mean
    row_var = jnp.mean(centered * centered, axis=-1, keepdims=True)
    normed = centered * lax.rsqrt(row_var + LN_EPS)
    return (normed * gain.astype(jnp.float32) + bias.astype(jnp.float32)).astype(jnp.bfloat16)


def rotary_tables(positions):
    inv_freq = 1.0 / (10000.0 ** (jnp.arange(0, ROT_DIM, 2).astype(jnp.float32) / ROT_DIM))
    angles = positions.astype(jnp.float32)[:, None] * inv_freq[None, :]
    return jnp.cos(angles)[:, None, :], jnp.sin(angles)[:, None, :]


def apply_rotary(vectors, cos_tab, sin_tab):
    lead_shape = vectors.shape[:-1]
    pairs = vectors[..., :ROT_DIM].reshape(lead_shape + (ROT_DIM // 2, 2))
    even_part = pairs[..., 0]
    odd_part = pairs[..., 1]
    rotated = jnp.stack([even_part * cos_tab - odd_part * sin_tab, odd_part * cos_tab + even_part * sin_tab], axis=-1)
    return jnp.concatenate([rotated.reshape(lead_shape + (ROT_DIM,)), vectors[..., ROT_DIM:]], axis=-1)


def attend(query, k_layer, v_layer, visible):
    score_scale = k_layer.shape[-1] ** -0.5
    scores = jnp.einsum("bhe,bshe->bhs", query, k_layer, preferred_element_type=jnp.float32) * score_scale
    scores = jnp.where(visible, scores, -jnp.inf)
    exp_scores = jnp.exp(scores - jnp.max(scores, axis=-1, keepdims=True))
    attn_probs = (exp_scores / jnp.sum(exp_scores, axis=-1, keepdims=True)).astype(jnp.bfloat16)
    context = jnp.einsum("bhs,bshe->bhe", attn_probs, v_layer, preferred_element_type=jnp.float32)
    return context.astype(jnp.bfloat16)


def step_setup(cur_len, step_idx, cache_len):
    new_pos = cur_len + step_idx
    slot_ids = jnp.arange(cache_len)
    visible = (slot_ids[None, :] <= new_pos[:, None])[:, None, :]
    return new_pos, rotary_tables(new_pos), visible


def layer_update(normed, new_pos, rotary, visible, caches, layer_idx, weights):
    cos_tab, sin_tab = rotary
    k_cache, v_cache = caches
    q_weight, k_weight, v_weight, o_weight, in_weight, in_bias, out_weight = weights
    batch = normed.shape[0]
    n_heads = k_cache.shape[3]
    head_dim = k_cache.shape[4]
    head_shape = (batch, n_heads, head_dim)
    query = jnp.dot(normed, q_weight, preferred_element_type=jnp.float32).reshape(head_shape)
    key_new = jnp.dot(normed, k_weight, preferred_element_type=jnp.float32).reshape(head_shape)
    value_new = jnp.dot(normed, v_weight, preferred_element_type=jnp.float32).astype(jnp.bfloat16).reshape(head_shape)
    query = apply_rotary(query, cos_tab, sin_tab).astype(jnp.bfloat16)
    key_new = apply_rotary(key_new, cos_tab, sin_tab).astype(jnp.bfloat16)
    batch_rows = jnp.arange(batch)
    k_cache = k_cache.at[layer_idx, batch_rows, new_pos].set(key_new)
    v_cache = v_cache.at[layer_idx, batch_rows, new_pos].set(value_new)
    context = attend(query, k_cache[layer_idx], v_cache[layer_idx], visible).reshape(batch, n_heads * head_dim)
    pre_act = jnp.dot(normed, in_weight, preferred_element_type=jnp.float32) + in_bias.astype(jnp.float32)
    gelu_act = jax.nn.gelu(pre_act, approximate=True).astype(jnp.bfloat16)
    layer_part = jnp.dot(context, o_weight, preferred_element_type=jnp.float32) + jnp.dot(gelu_act, out_weight, preferred_element_type=jnp.float32)
    return layer_part, k_cache, v_cache


def decode_shard(x_steps, cur_len, k_cache, v_cache, ln_gain, ln_bias, w_q, w_k, w_v, w_o, w_in, b_in, w_out, b_out):
    n_layers = k_cache.shape[0]
    outputs = []
    for step_idx in range(x_steps.shape[0]):
        new_pos, rotary, visible = step_setup(cur_len, step_idx, k_cache.shape[2])
        hidden = x_steps[step_idx]
        for layer_idx in range(n_layers):
            normed = layer_norm(hidden, ln_gain[layer_idx], ln_bias[layer_idx])
            weights = (w_q[layer_idx], w_k[layer_idx], w_v[layer_idx], w_o[layer_idx], w_in[layer_idx], b_in[layer_idx], w_out[layer_idx])
            layer_part, k_cache, v_cache = layer_update(normed, new_pos, rotary, visible, (k_cache, v_cache), layer_idx, weights)
            layer_sum = lax.psum(layer_part.astype(jnp.bfloat16), "tp")
            hidden = (hidden.astype(jnp.float32) + layer_sum.astype(jnp.float32) + b_out[layer_idx].astype(jnp.float32)).astype(jnp.bfloat16)
        outputs.append(hidden)
    return jnp.stack(outputs), k_cache, v_cache


def solution(mesh):
    cache_spec = P(None, "dp", None, "tp", None)
    in_specs = (P(None, "dp", None), P("dp"), cache_spec, cache_spec, P(None, None), P(None, None),
                P(None, None, "tp"), P(None, None, "tp"), P(None, None, "tp"), P(None, "tp", None),
                P(None, None, "tp"), P(None, "tp"), P(None, "tp", None), P(None, None))
    out_specs = (P(None, "dp", None), cache_spec, cache_spec)
    return jax.shard_map(decode_shard, mesh=mesh, in_specs=in_specs, out_specs=out_specs, check_vma=False)
```

profile of v0, /device:TPU:112, one launch (start us, length us, event | category | flops | bytes accessed | tf_op | source)
XLA Modules:
  0.0 3359.8 jit_solution(1990335605865432204)
XLA Ops:
  111.7 13.9 fusion.158
  133.4 15.0 fusion.156
  152.3 14.8 fusion.154
  170.9 14.9 fusion.152
  189.7 15.0 fusion.150
  208.6 14.8 fusion.148
  230.9 14.8 fusion.146
  249.6 14.9 fusion.144
  268.3 15.2 fusion.142
  287.4 14.8 fusion.140
  306.1 14.8 fusion.138
  324.8 14.8 fusion.136
  343.4 15.0 fusion.134
  362.3 14.8 fusion.132
  381.0 14.8 fusion.130
  399.7 15.0 fusion.128
  627.7 13.7 fusion.94
  677.5 10.5 slice_bitcast_fusion.58
  702.6 51.7 %all-reduce.21.cloned.1.call-done = bf16[64,4096]{1,0:T(8,128)(2,1)} async-done(((bf16[64,4096]{1,0:T(8,128)(2,1)}), bf16[64,4096]{1,0:T(8,128)(2,1)}) %all-reduce.21.cloned.1.call-update) | async-done | bytes 524304 | tf_op jit(solution)/shard_map/psum | solution.py:84
  763.2 13.7 fusion.92
  806.7 10.4 slice_bitcast_fusion.56
  852.7 10.5 slice_bitcast_fusion.54
  877.7 48.0 %all-reduce.23.cloned.1.call-done = bf16[64,4096]{1,0:T(8,128)(2,1)} async-done(((bf16[64,4096]{1,0:T(8,128)(2,1)}), bf16[64,4096]{1,0:T(8,128)(2,1)}) %all-reduce.23.cloned.1.call-update) | async-done | bytes 524304 | tf_op jit(solution)/shard_map/psum | solution.py:84
  934.6 13.9 fusion.90
  1024.3 10.5 slice_bitcast_fusion.50
  1049.2 48.1 %all-reduce.25.cloned.1.call-done = bf16[64,4096]{1,0:T(8,128)(2,1)} async-done(((bf16[64,4096]{1,0:T(8,128)(2,1)}), bf16[64,4096]{1,0:T(8,128)(2,1)}) %all-reduce.25.cloned.1.call-update) | async-done | bytes 524304 | tf_op jit(solution)/shard_map/psum | solution.py:84
  1106.3 13.9 fusion.88
  1195.9 10.5 slice_bitcast_fusion.46
  1220.9 48.1 %all-reduce.27.cloned.1.call-done = bf16[64,4096]{1,0:T(8,128)(2,1)} async-done(((bf16[64,4096]{1,0:T(8,128)(2,1)}), bf16[64,4096]{1,0:T(8,128)(2,1)}) %all-reduce.27.cloned.1.call-update) | async-done | bytes 524304 | tf_op jit(solution)/shard_map/psum | solution.py:84
  1277.9 13.9 fusion.86
  1367.7 10.5 slice_bitcast_fusion.42
  1393.4 48.1 %all-reduce.29.cloned.1.call-done = bf16[64,4096]{1,0:T(8,128)(2,1)} async-done(((bf16[64,4096]{1,0:T(8,128)(2,1)}), bf16[64,4096]{1,0:T(8,128)(2,1)}) %all-reduce.29.cloned.1.call-update) | async-done | bytes 524304 | tf_op jit(solution)/shard_map/psum | solution.py:84
  1450.4 13.9 fusion.84
  1540.9 10.5 slice_bitcast_fusion.38
  1566.5 48.1 %all-reduce.31.cloned.1.call-done = bf16[64,4096]{1,0:T(8,128)(2,1)} async-done(((bf16[64,4096]{1,0:T(8,128)(2,1)}), bf16[64,4096]{1,0:T(8,128)(2,1)}) %all-reduce.31.cloned.1.call-update) | async-done | bytes 524304 | tf_op jit(solution)/shard_map/psum | solution.py:84
  1623.6 13.9 fusion.82
  1714.0 10.5 slice_bitcast_fusion.34
  1739.7 48.1 %all-reduce.33.cloned.1.call-done = bf16[64,4096]{1,0:T(8,128)(2,1)} async-done(((bf16[64,4096]{1,0:T(8,128)(2,1)}), bf16[64,4096]{1,0:T(8,128)(2,1)}) %all-reduce.33.cloned.1.call-update) | async-done | bytes 524304 | tf_op jit(solution)/shard_map/psum | solution.py:84
  1796.7 13.9 fusion.80
  1887.2 10.5 slice_bitcast_fusion.30
  1912.8 48.1 %all-reduce.35.cloned.1.call-done = bf16[64,4096]{1,0:T(8,128)(2,1)} async-done(((bf16[64,4096]{1,0:T(8,128)(2,1)}), bf16[64,4096]{1,0:T(8,128)(2,1)}) %all-reduce.35.cloned.1.call-update) | async-done | bytes 524304 | tf_op jit(solution)/shard_map/psum | solution.py:84
  1969.9 13.9 fusion.78
  2060.3 10.5 slice_bitcast_fusion.26
  2086.0 48.1 %all-reduce.37.cloned.1.call-done = bf16[64,4096]{1,0:T(8,128)(2,1)} async-done(((bf16[64,4096]{1,0:T(8,128)(2,1)}), bf16[64,4096]{1,0:T(8,128)(2,1)}) %all-reduce.37.cloned.1.call-update) | async-done | bytes 524304 | tf_op jit(solution)/shard_map/psum | solution.py:84
  2143.0 13.9 fusion.76
  2233.5 10.5 slice_bitcast_fusion.22
  2259.2 48.1 %all-reduce.39.cloned.1.call-done = bf16[64,4096]{1,0:T(8,128)(2,1)} async-done(((bf16[64,4096]{1,0:T(8,128)(2,1)}), bf16[64,4096]{1,0:T(8,128)(2,1)}) %all-reduce.39.cloned.1.call-update) | async-done | bytes 524304 | tf_op jit(solution)/shard_map/psum | solution.py:84
  2316.2 13.9 fusion.74
  2406.7 10.5 slice_bitcast_fusion.18
  2432.3 48.1 %all-reduce.41.cloned.1.call-done = bf16[64,4096]{1,0:T(8,128)(2,1)} async-done(((bf16[64,4096]{1,0:T(8,128)(2,1)}), bf16[64,4096]{1,0:T(8,128)(2,1)}) %all-reduce.41.cloned.1.call-update) | async-done | bytes 524304 | tf_op jit(solution)/shard_map/psum | solution.py:84
  2489.4 13.9 fusion.72
  2579.8 10.5 slice_bitcast_fusion.14
  2605.5 48.1 %all-reduce.43.cloned.1.call-done = bf16[64,4096]{1,0:T(8,128)(2,1)} async-done(((bf16[64,4096]{1,0:T(8,128)(2,1)}), bf16[64,4096]{1,0:T(8,128)(2,1)}) %all-reduce.43.cloned.1.call-update) | async-done | bytes 524304 | tf_op jit(solution)/shard_map/psum | solution.py:84
  2662.5 13.9 fusion.70
  2753.0 10.5 slice_bitcast_fusion.10
  2778.7 48.1 %all-reduce.45.cloned.1.call-done = bf16[64,4096]{1,0:T(8,128)(2,1)} async-done(((bf16[64,4096]{1,0:T(8,128)(2,1)}), bf16[64,4096]{1,0:T(8,128)(2,1)}) %all-reduce.45.cloned.1.call-update) | async-done | bytes 524304 | tf_op jit(solution)/shard_map/psum | solution.py:84
  2835.7 13.9 fusion.68
  2926.2 10.5 slice_bitcast_fusion.6
  2951.8 48.1 %all-reduce.47.cloned.1.call-done = bf16[64,4096]{1,0:T(8,128)(2,1)} async-done(((bf16[64,4096]{1,0:T(8,128)(2,1)}), bf16[64,4096]{1,0:T(8,128)(2,1)}) %all-reduce.47.cloned.1.call-update) | async-done | bytes 524304 | tf_op jit(solution)/shard_map/psum | solution.py:84
  3008.8 13.9 fusion.66
  3099.3 10.5 slice_bitcast_fusion.2
  3125.0 48.1 %all-reduce.49.cloned.1.call-done = bf16[64,4096]{1,0:T(8,128)(2,1)} async-done(((bf16[64,4096]{1,0:T(8,128)(2,1)}), bf16[64,4096]{1,0:T(8,128)(2,1)}) %all-reduce.49.cloned.1.call-update) | async-done | bytes 524304 | tf_op jit(solution)/shard_map/psum | solution.py:84
  3185.4 13.7 fusion.64
  3243.9 95.3 %all-reduce.51.cloned.1.call-done = (bf16[64,4096]{1,0:T(8,128)(2,1)}, bf16[64,4096]{1,0:T(8,128)(2,1)}, bf16[64,4096]{1,0:T(8,128)(2,1)}, bf16[64,4096]{1,0:T(8...) async-done(((bf16[64,4096]{1,0:T(8,128)(2,1)}, ...) | async-done | bytes 8388624 | tf_op jit(solution)/shard_map/psum | solution.py:84
  (1664 shorter events, 1890.0 us)
Async XLA Ops:
  7.2 571.1 %all-reduce.19.cloned.1.call-start = ((), (), s32[]{:S(2)}) async-start(), calls=%async_computation | async-start | bytes 1048576 | tf_op jit(solution)/shard_map/psum | solution.py:84
  21.7 86.8 %copy-start.258 = (pred[64,64]{1,0:T(8,128)(4,1)}, pred[64,64]{1,0:T(8,128)(4,1)S(1)}, u32[]{:S(2)}) copy-start(pred[64,64]{1,0:T(8,128)(4,1)S(1)} %iota_compare_fusion.15) | copy-start | bytes 12292
  25.5 107.9 %copy-start.260 = (f32[64]{0:T(128)}, f32[64]{0:T(128)S(1)}, u32[]{:S(2)}) copy-start(f32[64]{0:T(128)S(1)} %get-tuple-element.426) | copy-start | bytes 772
  25.5 126.8 %copy-start.262 = (f32[64]{0:T(128)}, f32[64]{0:T(128)S(1)}, u32[]{:S(2)}) copy-start(f32[64]{0:T(128)S(1)} %get-tuple-element.425) | copy-start | bytes 772
  25.5 145.4 %copy-start.264 = (f32[64]{0:T(128)}, f32[64]{0:T(128)S(1)}, u32[]{:S(2)}) copy-start(f32[64]{0:T(128)S(1)} %get-tuple-element.424) | copy-start | bytes 772
  25.6 164.2 %copy-start.266 = (f32[64]{0:T(128)}, f32[64]{0:T(128)S(1)}, u32[]{:S(2)}) copy-start(f32[64]{0:T(128)S(1)} %get-tuple-element.423) | copy-start | bytes 772
  25.6 183.0 %copy-start.268 = (f32[64]{0:T(128)}, f32[64]{0:T(128)S(1)}, u32[]{:S(2)}) copy-start(f32[64]{0:T(128)S(1)} %get-tuple-element.422) | copy-start | bytes 772
  129.4 624.8 %all-reduce.21.cloned.1.call-start = ((), (), s32[]{:S(2)}) async-start(), calls=%async_computation.1 | async-start | bytes 1048576 | tf_op jit(solution)/shard_map/psum | solution.py:84
  474.3 27.5 slice-start.11
  475.6 27.7 slice-start.12
  475.6 29.3 slice-start.13
  475.6 30.9 slice-start.14
  477.7 31.6 slice-start.15
  478.4 45.9 %copy-start.175 = (bf16[64,2,192]{2,0,1:T(8,128)(2,1)S(1)}, bf16[64,2,192]{2,0,1:T(8,128)(2,1)}, u32[]{:S(2)}) copy-start(bf16[64,2,192]{2,0,1:T(8,128)(2,1)} %slice.3515) | copy-start | bytes 147460
  478.4 46.6 %copy-start.176 = (bf16[64,2,192]{2,0,1:T(8,128)(2,1)S(1)}, bf16[64,2,192]{2,0,1:T(8,128)(2,1)}, u32[]{:S(2)}) copy-start(bf16[64,2,192]{2,0,1:T(8,128)(2,1)} %slice.3514) | copy-start | bytes 147460
  479.8 45.3 %copy-start.174 = (bf16[64,2,192]{2,0,1:T(8,128)(2,1)S(1)}, bf16[64,2,192]{2,0,1:T(8,128)(2,1)}, u32[]{:S(2)}) copy-start(bf16[64,2,192]{2,0,1:T(8,128)(2,1)} %slice.3519) | copy-start | bytes 147460
  479.8 46.0 %copy-start.177 = (bf16[64,2,192]{2,0,1:T(8,128)(2,1)S(1)}, bf16[64,2,192]{2,0,1:T(8,128)(2,1)}, u32[]{:S(2)}) copy-start(bf16[64,2,192]{2,0,1:T(8,128)(2,1)} %slice.3518) | copy-start | bytes 147460
  479.8 47.6 %copy-start.178 = (bf16[64,2,192]{2,0,1:T(8,128)(2,1)S(1)}, bf16[64,2,192]{2,0,1:T(8,128)(2,1)}, u32[]{:S(2)}) copy-start(bf16[64,2,192]{2,0,1:T(8,128)(2,1)} %slice.3522) | copy-start | bytes 147460
  479.8 48.4 %copy-start.179 = (bf16[64,2,192]{2,0,1:T(8,128)(2,1)S(1)}, bf16[64,2,192]{2,0,1:T(8,128)(2,1)}, u32[]{:S(2)}) copy-start(bf16[64,2,192]{2,0,1:T(8,128)(2,1)} %slice.3526) | copy-start | bytes 147460
  479.8 50.0 %copy-start.180 = (bf16[64,2,192]{2,0,1:T(8,128)(2,1)S(1)}, bf16[64,2,192]{2,0,1:T(8,128)(2,1)}, u32[]{:S(2)}) copy-start(bf16[64,2,192]{2,0,1:T(8,128)(2,1)} %slice.3530) | copy-start | bytes 147460
  479.8 50.7 %copy-start.181 = (bf16[64,2,192]{2,0,1:T(8,128)(2,1)S(1)}, bf16[64,2,192]{2,0,1:T(8,128)(2,1)}, u32[]{:S(2)}) copy-start(bf16[64,2,192]{2,0,1:T(8,128)(2,1)} %slice.3534) | copy-start | bytes 147460
  479.9 51.5 %copy-start.182 = (bf16[64,2,192]{2,0,1:T(8,128)(2,1)S(1)}, bf16[64,2,192]{2,0,1:T(8,128)(2,1)}, u32[]{:S(2)}) copy-start(bf16[64,2,192]{2,0,1:T(8,128)(2,1)} %slice.3538) | copy-start | bytes 147460
  479.9 52.3 %copy-start.183 = (bf16[64,2,192]{2,0,1:T(8,128)(2,1)S(1)}, bf16[64,2,192]{2,0,1:T(8,128)(2,1)}, u32[]{:S(2)}) copy-start(bf16[64,2,192]{2,0,1:T(8,128)(2,1)} %slice.3542) | copy-start | bytes 147460
  479.9 53.9 %copy-start.184 = (bf16[64,2,192]{2,0,1:T(8,128)(2,1)S(1)}, bf16[64,2,192]{2,0,1:T(8,128)(2,1)}, u32[]{:S(2)}) copy-start(bf16[64,2,192]{2,0,1:T(8,128)(2,1)} %slice.3546) | copy-start | bytes 147460
  480.6 30.5 slice-start.16
  482.6 52.7 %copy-start.185 = (bf16[64,2,192]{2,0,1:T(8,128)(2,1)S(1)}, bf16[64,2,192]{2,0,1:T(8,128)(2,1)}, u32[]{:S(2)}) copy-start(bf16[64,2,192]{2,0,1:T(8,128)(2,1)} %slice.3550) | copy-start | bytes 147460
  484.0 52.1 %copy-start.186 = (bf16[64,2,192]{2,0,1:T(8,128)(2,1)S(1)}, bf16[64,2,192]{2,0,1:T(8,128)(2,1)}, u32[]{:S(2)}) copy-start(bf16[64,2,192]{2,0,1:T(8,128)(2,1)} %slice.3554) | copy-start | bytes 147460
  485.5 51.6 %copy-start.187 = (bf16[64,2,192]{2,0,1:T(8,128)(2,1)S(1)}, bf16[64,2,192]{2,0,1:T(8,128)(2,1)}, u32[]{:S(2)}) copy-start(bf16[64,2,192]{2,0,1:T(8,128)(2,1)} %slice.3558) | copy-start | bytes 147460
  486.2 29.3 copy-start.191
  486.9 27.9 copy-start.192
  487.6 49.7 %copy-start.188 = (bf16[64,2,192]{2,0,1:T(8,128)(2,1)S(1)}, bf16[64,2,192]{2,0,1:T(8,128)(2,1)}, u32[]{:S(2)}) copy-start(bf16[64,2,192]{2,0,1:T(8,128)(2,1)} %slice.3562) | copy-start | bytes 147460
  489.0 48.5 %copy-start.189 = (bf16[64,2,192]{2,0,1:T(8,128)(2,1)S(1)}, bf16[64,2,192]{2,0,1:T(8,128)(2,1)}, u32[]{:S(2)}) copy-start(bf16[64,2,192]{2,0,1:T(8,128)(2,1)} %slice.3566) | copy-start | bytes 147460
  489.9 47.8 %copy-start.190 = (bf16[64,2,192]{2,0,1:T(8,128)(2,1)S(1)}, bf16[64,2,192]{2,0,1:T(8,128)(2,1)}, u32[]{:S(2)}) copy-start(bf16[64,2,192]{2,0,1:T(8,128)(2,1)} %slice.3570) | copy-start | bytes 147460
  495.8 28.5 copy-start.238
  498.0 27.0 copy-start.239
  580.0 47.7 %copy-start.34 = (bf16[64,4096]{1,0:T(8,128)(2,1)}, bf16[64,4096]{1,0:T(8,128)(2,1)S(1)}, u32[]{:S(2)}) copy-start(bf16[64,4096]{1,0:T(8,128)(2,1)S(1)} %get-tuple-element.82) | copy-start | bytes 1572868
  597.5 30.1 copy-start.259
  698.4 227.2 %all-reduce.23.cloned.1.call-start = ((), (), s32[]{:S(2)}) async-start(), calls=%async_computation.2 | async-start | bytes 1048576 | tf_op jit(solution)/shard_map/psum | solution.py:84
  873.7 223.6 %all-reduce.25.cloned.1.call-start = ((), (), s32[]{:S(2)}) async-start(), calls=%async_computation.3 | async-start | bytes 1048576 | tf_op jit(solution)/shard_map/psum | solution.py:84
  1045.3 223.7 %all-reduce.27.cloned.1.call-start = ((), (), s32[]{:S(2)}) async-start(), calls=%async_computation.4 | async-start | bytes 1048576 | tf_op jit(solution)/shard_map/psum | solution.py:84
  1216.9 224.5 %all-reduce.29.cloned.1.call-start = ((), (), s32[]{:S(2)}) async-start(), calls=%async_computation.5 | async-start | bytes 1048576 | tf_op jit(solution)/shard_map/psum | solution.py:84
  1389.4 225.2 %all-reduce.31.cloned.1.call-start = ((), (), s32[]{:S(2)}) async-start(), calls=%async_computation.6 | async-start | bytes 1048576 | tf_op jit(solution)/shard_map/psum | solution.py:84
  1504.8 26.8 copy-start.170
  1562.6 225.2 %all-reduce.33.cloned.1.call-start = ((), (), s32[]{:S(2)}) async-start(), calls=%async_computation.7 | async-start | bytes 1048576 | tf_op jit(solution)/shard_map/psum | solution.py:84
  1678.0 26.8 copy-start.168
  1735.7 225.2 %all-reduce.35.cloned.1.call-start = ((), (), s32[]{:S(2)}) async-start(), calls=%async_computation.8 | async-start | bytes 1048576 | tf_op jit(solution)/shard_map/psum | solution.py:84
  1851.1 26.8 copy-start.166
  1908.9 225.2 %all-reduce.37.cloned.1.call-start = ((), (), s32[]{:S(2)}) async-start(), calls=%async_computation.9 | async-start | bytes 1048576 | tf_op jit(solution)/shard_map/psum | solution.py:84
  2024.3 26.8 copy-start.164
  2082.0 225.2 %all-reduce.39.cloned.1.call-start = ((), (), s32[]{:S(2)}) async-start(), calls=%async_computation.10 | async-start | bytes 1048576 | tf_op jit(solution)/shard_map/psum | solution.py:84
  2255.2 225.2 %all-reduce.41.cloned.1.call-start = ((), (), s32[]{:S(2)}) async-start(), calls=%async_computation.11 | async-start | bytes 1048576 | tf_op jit(solution)/shard_map/psum | solution.py:84
  2428.4 225.2 %all-reduce.43.cloned.1.call-start = ((), (), s32[]{:S(2)}) async-start(), calls=%async_computation.12 | async-start | bytes 1048576 | tf_op jit(solution)/shard_map/psum | solution.py:84
  2543.8 26.8 copy-start.158
  2601.5 225.2 %all-reduce.45.cloned.1.call-start = ((), (), s32[]{:S(2)}) async-start(), calls=%async_computation.13 | async-start | bytes 1048576 | tf_op jit(solution)/shard_map/psum | solution.py:84
  2774.7 225.2 %all-reduce.47.cloned.1.call-start = ((), (), s32[]{:S(2)}) async-start(), calls=%async_computation.14 | async-start | bytes 1048576 | tf_op jit(solution)/shard_map/psum | solution.py:84
  2947.8 225.2 %all-reduce.49.cloned.1.call-start = ((), (), s32[]{:S(2)}) async-start(), calls=%async_computation.15 | async-start | bytes 1048576 | tf_op jit(solution)/shard_map/psum | solution.py:84
  3121.0 218.2 %all-reduce.51.cloned.1.call-start = ((), (), s32[]{:S(2)}) async-start(), calls=%async_computation.16 | async-start | bytes 16777216 | tf_op jit(solution)/shard_map/psum | solution.py:84
  3239.8 99.5 %copy-start.35 = (bf16[64,4096]{1,0:T(8,128)(2,1)S(1)}, bf16[64,4096]{1,0:T(8,128)(2,1)}, u32[]{:S(2)}) copy-start(bf16[64,4096]{1,0:T(8,128)(2,1)} %copy-done.34) | copy-start | bytes 1572868
  3239.8 99.5 %copy-start.98 = (f32[1,4096]{1,0:T(1,128)S(1)}, f32[1,4096]{1,0:T(1,128)}, u32[]{:S(2)}) copy-start(f32[1,4096]{1,0:T(1,128)} %get-tuple-element.279) | copy-start | bytes 49156
  3239.8 100.9 %copy-start.37 = (bf16[64,4096]{1,0:T(8,128)(2,1)S(1)}, bf16[64,4096]{1,0:T(8,128)(2,1)}, u32[]{:S(2)}) copy-start(bf16[64,4096]{1,0:T(8,128)(2,1)} %copy-done.36) | copy-start | bytes 1572868
  3239.9 102.6 %copy-start.39 = (bf16[64,4096]{1,0:T(8,128)(2,1)S(1)}, bf16[64,4096]{1,0:T(8,128)(2,1)}, u32[]{:S(2)}) copy-start(bf16[64,4096]{1,0:T(8,128)(2,1)} %copy-done.38) | copy-start | bytes 1572868
  3239.9 103.9 %copy-start.41 = (bf16[64,4096]{1,0:T(8,128)(2,1)S(1)}, bf16[64,4096]{1,0:T(8,128)(2,1)}, u32[]{:S(2)}) copy-start(bf16[64,4096]{1,0:T(8,128)(2,1)} %copy-done.40) | copy-start | bytes 1572868
  3243.8 101.3 %copy-start.43 = (bf16[64,4096]{1,0:T(8,128)(2,1)S(1)}, bf16[64,4096]{1,0:T(8,128)(2,1)}, u32[]{:S(2)}) copy-start(bf16[64,4096]{1,0:T(8,128)(2,1)} %copy-done.42) | copy-start | bytes 1572868
  3243.8 102.6 %copy-start.45 = (bf16[64,4096]{1,0:T(8,128)(2,1)S(1)}, bf16[64,4096]{1,0:T(8,128)(2,1)}, u32[]{:S(2)}) copy-start(bf16[64,4096]{1,0:T(8,128)(2,1)} %copy-done.44) | copy-start | bytes 1572868
  (274 other events, 3759.1 us)
Sparse Core Ops, SparseCore 0:
  129.6 55.7 all-reduce.18
  698.6 55.6 all-reduce.20
  873.8 51.7 all-reduce.22
  1045.4 51.8 all-reduce.24
  1217.0 51.8 all-reduce.26
  1389.5 51.8 all-reduce.28
  1562.7 51.8 all-reduce.30
  1735.8 51.8 all-reduce.32
  1909.0 51.8 all-reduce.34
  2082.2 51.8 all-reduce.36
  2255.3 51.8 all-reduce.38
  2428.5 51.8 all-reduce.40
  2601.6 51.8 all-reduce.42
  2774.8 51.8 all-reduce.44
  2948.0 51.8 all-reduce.46
  3121.1 51.8 all-reduce.48
  3244.0 95.1 all-reduce.50
where the time goes:
time: 3380 us; the launch traced here: 3360 us
  local copies, waits for them, and re-layouts  1380 us (41%)
  matrix products  1010 us (30%)
  waiting for transfers between devices  821 us (24%)
  other arithmetic  124 us (4%)
    psum x17, waiting for transfers between devices, decode_shard(): layer_sum = lax.psum(layer_part.astype(jnp.bfloat16), 'tp')  820 us
    dot_general x32, matrix products, layer_update(): jnp.dot(gelu_act, out_weight, preferred_element_type=jnp.float32)  460 us
    squeeze x32, local copies, waits for them, and re-layouts, layer_update(): v_cache[layer_idx]  335 us
    squeeze x32, local copies, waits for them, and re-layouts, layer_update(): k_cache[layer_idx]  327 us
    scatter x32, local copies, waits for them, and re-layouts, layer_update(): v_cache = v_cache.at[layer_idx, batch_rows, new_pos].set(value_new)  299 us
    scatter x32, local copies, waits for them, and re-layouts, layer_update(): k_cache = k_cache.at[layer_idx, batch_rows, new_pos].set(key_new)  292 us
    dot_general x32, matrix products, layer_update(): jnp.dot(context, o_weight, preferred_element_type=jnp.float32)  125 us
    dot_general x32, matrix products, layer_update(): jnp.dot(normed, v_weight, preferred_element_type=jnp.float32)  122 us
  transfers between devices with their start and end apart: 17, of which 16 were waited for; matrix products, arithmetic and copies ran while one was open for 15% of the time, Pallas kernels for 0%

commit v1 on v0

v1 whole, which is shorter than its diff:
```python
import jax
import jax.numpy as jnp
from jax import lax
from jax.sharding import PartitionSpec as P

ROT_DIM = 64
LN_EPS = 1e-5


def layer_norm(hidden, gain, bias):
    hid_f32 = hidden.astype(jnp.float32)
    row_mean = jnp.mean(hid_f32, axis=-1, keepdims=True)
    centered = hid_f32 - row_mean
    row_var = jnp.mean(centered * centered, axis=-1, keepdims=True)
    normed = centered * lax.rsqrt(row_var + LN_EPS)
    return (normed * gain.astype(jnp.float32) + bias.astype(jnp.float32)).astype(jnp.bfloat16)


def rotary_rows(positions, head_dim, n_heads):
    inv_freq = 1.0 / (10000.0 ** (jnp.arange(0, ROT_DIM, 2).astype(jnp.float32) / ROT_DIM))
    angles = positions.astype(jnp.float32)[:, None] * inv_freq[None, :]
    rows = positions.shape[0]
    cos_pair = jnp.repeat(jnp.cos(angles), 2, axis=1)
    sin_pair = jnp.repeat(jnp.sin(angles), 2, axis=1) * jnp.where(jnp.arange(ROT_DIM) % 2 == 0, -1.0, 1.0)[None, :]
    cos_head = jnp.concatenate([cos_pair, jnp.ones((rows, head_dim - ROT_DIM), jnp.float32)], axis=1)
    sin_head = jnp.concatenate([sin_pair, jnp.zeros((rows, head_dim - ROT_DIM), jnp.float32)], axis=1)
    return jnp.tile(cos_head, (1, n_heads)), jnp.tile(sin_head, (1, n_heads))


def apply_rotary(vectors, cos_tab, sin_tab):
    even = (jnp.arange(vectors.shape[-1]) % 2 == 0)[None, :]
    partner = jnp.where(even, jnp.roll(vectors, -1, axis=-1), jnp.roll(vectors, 1, axis=-1))
    return (vectors * cos_tab + partner * sin_tab).astype(jnp.bfloat16)


def decode_shard(x_steps, cur_len, k_cache, v_cache, ln_gain, ln_bias, w_q, w_k, w_v, w_o, w_in, b_in, w_out, b_out):
    n_steps, batch, d_model = x_steps.shape
    n_layers, _, cache_len, n_heads, head_dim = k_cache.shape
    rows = n_steps * batch
    steps = jnp.arange(n_steps)
    positions = cur_len[None, :] + steps[:, None]
    cos_tab, sin_tab = rotary_rows(positions.reshape(rows), head_dim, n_heads)
    slots = jnp.arange(cache_len)
    visible = slots[None, None, None, :] <= positions[:, :, None, None]
    place = slots[None, :, None] == positions.T[:, None, :]
    written = jnp.any(place, axis=2)[:, :, None, None]
    place = place.astype(jnp.bfloat16)

    def put(old, new):
        spread = jnp.einsum("bst,tbn->bsn", place, new.reshape(n_steps, batch, n_heads * head_dim),
                            preferred_element_type=jnp.float32).astype(jnp.bfloat16)
        return jnp.where(written, spread.reshape(old.shape), old)

    hidden = x_steps.reshape(rows, d_model)
    k_out, v_out = [], []
    for layer in range(n_layers):
        normed = layer_norm(hidden, ln_gain[layer], ln_bias[layer])
        query = jnp.dot(normed, w_q[layer], preferred_element_type=jnp.float32)
        key_new = jnp.dot(normed, w_k[layer], preferred_element_type=jnp.float32)
        value_new = jnp.dot(normed, w_v[layer], preferred_element_type=jnp.float32).astype(jnp.bfloat16)
        query = apply_rotary(query, cos_tab, sin_tab).reshape(n_steps, batch, n_heads, head_dim)
        key_new = apply_rotary(key_new, cos_tab, sin_tab)
        keys = put(k_cache[layer], key_new)
        values = put(v_cache[layer], value_new)
        k_out.append(keys)
        v_out.append(values)
        scores = jnp.einsum("tbhe,bshe->tbhs", query, keys, preferred_element_type=jnp.float32) * (head_dim ** -0.5)
        scores = jnp.where(visible, scores, -jnp.inf)
        exp_scores = jnp.exp(scores - jnp.max(scores, axis=-1, keepdims=True))
        probs = (exp_scores / jnp.sum(exp_scores, axis=-1, keepdims=True)).astype(jnp.bfloat16)
        context = jnp.einsum("tbhs,bshe->tbhe", probs, values, preferred_element_type=jnp.float32)
        context = context.astype(jnp.bfloat16).reshape(rows, n_heads * head_dim)
        pre_act = jnp.dot(normed, w_in[layer], preferred_element_type=jnp.float32) + b_in[layer].astype(jnp.float32)
        gelu_act = jax.nn.gelu(pre_act, approximate=True).astype(jnp.bfloat16)
        part = jnp.dot(context, w_o[layer], preferred_element_type=jnp.float32) + jnp.dot(
            gelu_act, w_out[layer], preferred_element_type=jnp.float32)
        total = lax.psum(part.astype(jnp.bfloat16), "tp")
        hidden = (hidden.astype(jnp.float32) + total.astype(jnp.float32) + b_out[layer].astype(jnp.float32)).astype(jnp.bfloat16)
    return hidden.reshape(n_steps, batch, d_model), jnp.stack(k_out), jnp.stack(v_out)


def solution(mesh):
    cache_spec = P(None, "dp", None, "tp", None)
    in_specs = (P(None, "dp", None), P("dp"), cache_spec, cache_spec, P(None, None), P(None, None),
                P(None, None, "tp"), P(None, None, "tp"), P(None, None, "tp"), P(None, "tp", None),
                P(None, None, "tp"), P(None, "tp"), P(None, "tp", None), P(None, None))
    out_specs = (P(None, "dp", None), cache_spec, cache_spec)
    return jax.shard_map(decode_shard, mesh=mesh, in_specs=in_specs, out_specs=out_specs, check_vma=False)
```

time: 3380 us -> 569 us (0.17)
  local copies, waits for them, and re-layouts: 1380 us -> 80.1 us
  matrix products: 1010 us -> 206 us
  waiting for transfers between devices: 821 us -> 127 us
    dot_general x224 -> x20, matrix products: 1010 us -> 206 us  [the longest x2 56.8 us: decode_shard(): jnp.dot(gelu_act, w_out[layer], preferred_element_type=jnp.float32)]
    psum x17 -> x2, waiting for transfers between devices: 820 us -> 127 us  [decode_shard(): total = lax.psum(part.astype(jnp.bfloat16), 'tp')]
    squeeze x64 -> x0, local copies, waits for them, and re-layouts: 662 us -> none  [the longest x32 335 us: layer_update(): v_cache[layer_idx]]
    scatter x64 -> x0, local copies, waits for them, and re-layouts: 591 us -> none  [the longest x32 299 us: layer_update(): v_cache = v_cache.at[layer_idx, batch_rows, new_pos].set(value_new)]
    select_n x0 -> x4, other arithmetic: none -> 54.7 us  [the longest x3 54.7 us: put(): return jnp.where(written, spread.reshape(old.shape), old)]
    dot_general x38 -> x0, local copies, waits for them, and re-layouts: 37.3 us -> none  [the longest x3 18.7 us: layer_update(): jnp.dot(normed, k_weight, preferred_element_type=jnp.float32)]
  transfers between devices with their start and end apart: 17 -> 2, of which waited for: 16 -> 2; matrix products, arithmetic and copies ran while one was open for 15% -> 12% of each run, Pallas kernels for 0% -> 0%
where the time goes in v1:
time: 569 us; the launch traced here: 564 us
  matrix products  206 us (36%)
  other arithmetic  136 us (24%)
  waiting for transfers between devices  127 us (22%)
  local copies, waits for them, and re-layouts  80.1 us (14%)
  between operations  14.8 us (3%)
    psum x2, waiting for transfers between devices, decode_shard(): total = lax.psum(part.astype(jnp.bfloat16), 'tp')  127 us
    dot_general x2, matrix products, decode_shard(): jnp.dot(gelu_act, w_out[layer], preferred_element_type=jnp.float32)  56.8 us
    reshape x8, local copies, waits for them, and re-layouts, put(): return jnp.where(written, spread.reshape(old.shape), old)  55.6 us
    select_n x3, other arithmetic, put(): return jnp.where(written, spread.reshape(old.shape), old)  54.7 us
    dot_general x2, matrix products, decode_shard(): jnp.dot(normed, w_in[layer], preferred_element_type=jnp.float32)  45.7 us
    dot_general x2, matrix products, decode_shard(): jnp.dot(context, w_o[layer], preferred_element_type=jnp.float32)  23.1 us
    dot_general x4, matrix products, put(): jnp.einsum('bst,tbn->bsn', place, new.reshape(n_steps, batch, n_heads * h...  21.4 us
    dot_general x2, matrix products, decode_shard(): jnp.dot(normed, w_v[layer], preferred_element_type=jnp.float32)  15.7 us
  transfers between devices with their start and end apart: 2, of which 2 were waited for; matrix products, arithmetic and copies ran while one was open for 12% of the time, Pallas kernels for 0%

profile of v1, /device:TPU:112, one launch (start us, length us, event | category | flops | bytes accessed | tf_op | source)
XLA Modules:
  0.0 564.1 jit_solution(6611581530498323118)
XLA Ops:
  7.3 0.8 iota_add_fusion.1
  8.1 0.9 iota_add_fusion
  9.0 5.3 convert_reduce_fusion.1
  14.3 2.3 multiply_reduce_fusion
  16.6 0.6 slice_convert_fusion.2
  17.9 4.4 add_convert_fusion.2
  22.3 8.1 %fusion.50 = f32[1024,512]{0,1:T(8,128)S(1)} fusion(bf16[1024,4096]{1,0:T(8,128)(2,1)S(1)} %bitcast.145, bf16[2,4096,512]{2,1,0:T(8,128)(2,1)} %param.20), kind=kOutput, calls=%fused_computation.77 | convolution fusion | flops 4294967296 | bytes 14680064 | tf_op jit(solution)/shard_map/dot_general | solution.py:58
  30.4 6.5 %fusion.52 = f32[1024,512]{0,1:T(8,128)S(1)} fusion(bf16[1024,4096]{1,0:T(8,128)(2,1)S(1)} %bitcast.146, bf16[2,4096,512]{2,1,0:T(8,128)(2,1)} %param.21), kind=kOutput, calls=%fused_computation.79 | convolution fusion | flops 4294967296 | bytes 14680064 | tf_op jit(solution)/shard_map/dot_general | solution.py:59
  36.9 4.0 fusion.162
  41.9 0.9 iota_compare_fusion
  43.7 0.9 reshape.287
  44.6 9.1 %fusion.90 = bf16[1024,512]{1,0:T(8,128)(2,1)S(1)} fusion(bf16[1024,4096]{1,0:T(8,128)(2,1)} %bitcast.147, bf16[2,4096,512]{2,1,0:T(8,128)(2,1)} %param.22), kind=kOutput, calls=%fused_computation.125 | convolution fusion | flops 4295491584 | bytes 13631488 | tf_op jit(solution)/shard_map/dot_general | solution.py:60
  53.6 24.2 %fusion.16 = f32[1024,2048]{1,0:T(8,128)} fusion(bf16[1024,4096]{1,0:T(8,128)(2,1)} %bitcast.148, bf16[2,4096,2048]{2,1,0:T(8,128)(2,1)} %param.24), kind=kOutput, calls=%fused_computation.19 | convolution fusion | flops 17179869184 | bytes 33554432 | tf_op jit(solution)/shard_map/dot_general | solution.py:73
  77.8 5.0 convolution_convert_fusion.3
  82.8 6.9 %reshape.285 = bf16[64,64,2,256]{3,2,1,0:T(2,128)(2,1)} reshape(bf16[64,64,512]{2,1,0:T(8,128)(2,1)} %convolution_convert_fusion.3) | data formatting | bytes 8388608 | tf_op jit(solution)/shard_map/reshape | solution.py:52
  89.7 1.0 broadcast_multiply_fusion
  91.0 6.1 %fusion.83 = (bf16[1024,512]{0,1:T(8,128)(2,1)}, bf16[1024,512]{0,1:T(8,128)(2,1)S(1)}) fusion(f32[1024,512]{0,1:T(8,128)} %copy-done.3, f32[1024,1]{0,1:T(1,128)S(1)} %get-tuple-element.22, f32[1024,511]{0,1:T(8,128)} %get-tuple-element.24, f32[1024,511]{0,1:T(8,128)} %get-tuple-element.23, f32[1024,1]{0,1:T(1,128)S(1)} %get-tuple-element.21, ...), kind=kLoop, calls=%fused_computation.114 | loop fusion | flops 7340032 | bytes 16777728 | tf_op jit(solution)/shard_map/convert_element_type | solution.py:33
  97.1 2.3 copy.29
  99.4 1.3 reshape.312
  100.7 2.7 copy.33
  103.4 6.3 %convolution_convert_fusion.2 = bf16[64,64,512]{2,1,0:T(8,128)(2,1)} fusion(bf16[16,64,512]{2,1,0:T(8,128)(2,1)} %bitcast.150, s32[64,16]{1,0:T(8,128)S(1)} %iota_add_fusion), kind=kOutput, calls=%fused_computation.111 | convolution fusion | flops 69271552 | bytes 5246976 | tf_op jit(solution)/shard_map/bst,tbn->bsn/dot_general | solution.py:50
  109.7 6.9 %reshape.289 = bf16[64,64,2,256]{3,2,1,0:T(2,128)(2,1)} reshape(bf16[64,64,512]{2,1,0:T(8,128)(2,1)} %convolution_convert_fusion.2) | data formatting | bytes 8388608 | tf_op jit(solution)/shard_map/reshape | solution.py:52
  116.6 14.7 %broadcast_select_fusion.6 = (bf16[64,64,2,256]{3,2,1,0:T(2,128)(2,1)S(1)}, bf16[64,64,2,256]{3,2,1,0:T(2,128)(2,1)}) fusion(bf16[64,64,2,256]{3,2,1,0:T(2,128)(2,1)} %reshape.289, pred[64,64]{1,0:T(8,128)(4,1)S(1)} %fusion.136, bf16[2,64,64,2,256]{4,3,2,1,0:T(2,128)(2,1)} %param.16, bf16[64,64,2,256]{3,2,1,0:T(2,128)(2,1)} %reshape.285, ...), kind=kLoop, calls=%fused_computation.59 | loop fusion | flops 4194304 | bytes 25169920 | tf_op jit(solution)/shard_map/jit(_where)/select_n | solution.py:52
  131.3 1.2 fusion.127
  132.5 0.8 fusion.165
  133.2 5.9 %fusion.109 = bf16[16,64,2,256]{3,0,2,1:T(8,128)(2,1)S(1)} fusion(bf16[64,64,2,256]{3,2,1,0:T(2,128)(2,1)} %get-tuple-element.42, f32[16,64,2]{0,2,1:T(2,128)S(1)} %fusion.165, f32[16,64,2,64]{3,0,2,1:T(8,128)S(1)} %fusion.127), kind=kOutput, calls=%fused_computation.134 | convolution fusion | flops 68028480 | bytes 5775360 | tf_op jit(solution)/shard_map/tbhs,bshe->tbhe/dot_general | solution.py:71
  139.1 1.0 copy.35
  140.4 28.3 %fusion.14 = f32[1024,4096]{1,0:T(8,128)} fusion(bf16[2,2048,4096]{2,1,0:T(8,128)(2,1)} %param.26, f32[1024,2048]{1,0:T(8,128)} %fusion.16, f32[2048]{0:T(1024)S(1)} %bitcast.165), kind=kOutput, calls=%fused_computation.17 | convolution fusion | flops 17200840704 | bytes 41951232 | tf_op jit(solution)/shard_map/dot_general | solution.py:75
  168.7 11.6 %add_convert_fusion.1 = bf16[1024,4096]{1,0:T(8,128)(2,1)} fusion(f32[1024,4096]{1,0:T(8,128)} %fusion.14, bf16[1024,512]{1,0:T(8,128)(2,1)S(1)} %bitcast.157, bf16[2,512,4096]{2,1,0:T(8,128)(2,1)} %param.23), kind=kOutput, calls=%fused_computation.27 | convolution fusion | flops 4303355904 | bytes 30408704 | tf_op jit(solution)/shard_map/dot_general | solution.py:75
  180.4 7.1 %reshape.301 = bf16[1,64,64,2,256]{4,3,2,1,0:T(2,128)(2,1)} reshape(bf16[64,64,512]{2,1,0:T(8,128)(2,1)} %convolution_convert_fusion.3) | data formatting | bytes 8388608 | tf_op jit(solution)/shard_map/reshape | solution.py:52
  187.5 6.9 %reshape.299 = bf16[1,64,64,2,256]{4,3,2,1,0:T(2,128)(2,1)} reshape(bf16[64,64,512]{2,1,0:T(8,128)(2,1)} %convolution_convert_fusion.2) | data formatting | bytes 8388608 | tf_op jit(solution)/shard_map/reshape | solution.py:52
  194.4 0.6 slice_convert_fusion
  195.0 84.1 %all-reduce.5.cloned.1.call-done = bf16[1024,4096]{1,0:T(8,128)(2,1)} async-done(((bf16[1024,4096]{1,0:T(8,128)(2,1)}), bf16[1024,4096]{1,0:T(8,128)(2,1)}) %all-reduce.5.cloned.1.call-update) | async-done | bytes 8388624 | tf_op jit(solution)/shard_map/psum | solution.py:77
  279.2 7.6 %convert_reduce_fusion = (f32[1024]{0:T(1024)S(1)}, bf16[1024,4096]{1,0:T(8,128)(2,1)S(1)}) fusion(f32[4096]{0:T(1024)S(1)} %bitcast.158, bf16[1024,4096]{1,0:T(8,128)(2,1)} %all-reduce.5.cloned.1.call-done, bf16[16,64,4096]{2,1,0:T(8,128)(2,1)} %param.14), kind=kLoop, calls=%fused_computation.4 | loop fusion | flops 29359104 | bytes 25186304 | tf_op jit(solution)/shard_map/reduce_sum | solution.py:12
  286.8 2.3 fusion.4
  289.1 4.6 fusion.7
  293.7 6.7 %fusion.93 = bf16[1024,512]{1,0:T(8,128)(2,1)S(1)} fusion(bf16[1024,4096]{1,0:T(8,128)(2,1)S(1)} %fusion.7, bf16[2,4096,512]{2,1,0:T(8,128)(2,1)} %param.22), kind=kOutput, calls=%fused_computation.126 | convolution fusion | flops 4295491584 | bytes 13631488 | tf_op jit(solution)/shard_map/dot_general | solution.py:60
  300.4 6.7 %fusion.43 = f32[1024,512]{0,1:T(8,128)S(1)} fusion(bf16[1024,4096]{1,0:T(8,128)(2,1)S(1)} %fusion.7, bf16[2,4096,512]{2,1,0:T(8,128)(2,1)} %param.20), kind=kOutput, calls=%fused_computation.70 | convolution fusion | flops 4294967296 | bytes 14680064 | tf_op jit(solution)/shard_map/dot_general | solution.py:58
  307.1 8.2 %fusion.45 = f32[1024,512]{0,1:T(8,128)} fusion(bf16[1024,4096]{1,0:T(8,128)(2,1)S(1)} %fusion.7, bf16[2,4096,512]{2,1,0:T(8,128)(2,1)} %param.21), kind=kOutput, calls=%fused_computation.72 | convolution fusion | flops 4294967296 | bytes 14680064 | tf_op jit(solution)/shard_map/dot_general | solution.py:59
  315.3 21.5 %fusion.12 = f32[1024,2048]{1,0:T(8,128)} fusion(bf16[1024,4096]{1,0:T(8,128)(2,1)S(1)} %fusion.7, bf16[2,4096,2048]{2,1,0:T(8,128)(2,1)} %param.24), kind=kOutput, calls=%fused_computation.15 | convolution fusion | flops 17179869184 | bytes 33554432 | tf_op jit(solution)/shard_map/dot_general | solution.py:73
  336.8 5.1 convolution_convert_fusion.1
  341.9 6.9 %reshape.302 = bf16[1,64,64,2,256]{4,3,2,1,0:T(2,128)(2,1)} reshape(bf16[64,64,512]{2,1,0:T(8,128)(2,1)} %convolution_convert_fusion.1) | data formatting | bytes 8388608 | tf_op jit(solution)/shard_map/reshape | solution.py:52
  348.8 6.9 %reshape.293 = bf16[64,64,2,256]{3,2,1,0:T(2,128)(2,1)} reshape(bf16[64,64,512]{2,1,0:T(8,128)(2,1)} %convolution_convert_fusion.1) | data formatting | bytes 8388608 | tf_op jit(solution)/shard_map/reshape | solution.py:52
  355.8 0.8 fusion.157
  356.6 2.8 fusion.158
  360.0 2.2 fusion.87
  362.1 1.9 copy.37
  364.0 5.1 convolution_convert_fusion
  369.1 6.9 %reshape.300 = bf16[1,64,64,2,256]{4,3,2,1,0:T(2,128)(2,1)} reshape(bf16[64,64,512]{2,1,0:T(8,128)(2,1)} %convolution_convert_fusion) | data formatting | bytes 8388608 | tf_op jit(solution)/shard_map/reshape | solution.py:52
  376.1 7.0 %reshape.295 = bf16[64,64,2,256]{3,2,1,0:T(2,128)(2,1)} reshape(bf16[64,64,512]{2,1,0:T(8,128)(2,1)} %convolution_convert_fusion) | data formatting | bytes 8388608 | tf_op jit(solution)/shard_map/reshape | solution.py:52
  383.1 1.3 reshape.313
  384.4 2.7 copy.41
  387.1 14.3 %broadcast_select_fusion.4 = (bf16[64,64,2,256]{3,2,1,0:T(2,128)(2,1)S(1)}, bf16[64,64,2,256]{3,2,1,0:T(2,128)(2,1)}) fusion(bf16[64,64,2,256]{3,2,1,0:T(2,128)(2,1)} %reshape.295, pred[64,64]{1,0:T(8,128)(4,1)S(1)} %copy-done.14, bf16[2,64,64,2,256]{4,3,2,1,0:T(2,128)(2,1)} %param.16, bf16[64,64,2,256]{3,2,1,0:T(2,128)(2,1)} %reshape.293, ...), kind=kLoop, calls=%fused_computation.57 | loop fusion | flops 4194304 | bytes 25169920 | tf_op jit(solution)/shard_map/jit(_where)/select_n | solution.py:52
  401.4 1.2 fusion.124
  402.6 0.8 fusion.166
  403.4 5.9 %fusion.106 = bf16[16,64,2,256]{3,0,2,1:T(8,128)(2,1)S(1)} fusion(bf16[64,64,2,256]{3,2,1,0:T(2,128)(2,1)} %get-tuple-element.38, f32[16,64,2]{0,2,1:T(2,128)S(1)} %fusion.166, f32[16,64,2,64]{3,0,2,1:T(8,128)S(1)} %fusion.124), kind=kOutput, calls=%fused_computation.133 | convolution fusion | flops 68028480 | bytes 5775360 | tf_op jit(solution)/shard_map/tbhs,bshe->tbhe/dot_general | solution.py:71
  409.2 1.0 copy.43
  410.5 28.5 %fusion.10 = f32[1024,4096]{1,0:T(8,128)} fusion(bf16[2,2048,4096]{2,1,0:T(8,128)(2,1)} %param.26, f32[1024,2048]{1,0:T(8,128)} %fusion.12, f32[2048]{0:T(1024)S(1)} %bitcast.164), kind=kOutput, calls=%fused_computation.13 | convolution fusion | flops 17200840704 | bytes 41951232 | tf_op jit(solution)/shard_map/dot_general | solution.py:75
  439.0 11.5 %add_convert_fusion = bf16[1024,4096]{1,0:T(8,128)(2,1)} fusion(f32[1024,4096]{1,0:T(8,128)} %fusion.10, bf16[1024,512]{1,0:T(8,128)(2,1)S(1)} %bitcast.156, bf16[2,512,4096]{2,1,0:T(8,128)(2,1)} %param.23), kind=kOutput, calls=%fused_computation.24 | convolution fusion | flops 4303355904 | bytes 30408704 | tf_op jit(solution)/shard_map/dot_general | solution.py:75
  450.5 25.8 %broadcast_select_fusion.1 = (bf16[1,64,64,2,256]{4,3,2,1,0:T(2,128)(2,1)S(1)}, bf16[1,64,64,2,256]{4,3,2,1,0:T(2,128)(2,1)S(1)}, bf16[1,64,64,2,256]{4,3,2,1,0:T(2,128)(2,1)S(1)}, bf16[1,64,64,2,256]{4,3,2,1,0:T(2,128)(2,1)S(1)}) fusion(bf16[1,64,64,2,256]{4,3,2,1,0:T(2,128)(2,1)} %reshape.301, pred[64,64]{1,0:T(8,128)(4,1)S(1)} %copy-done.14, ...), kind=kLoop, calls=%fused_computation.54 | loop fusion | flops 8388608 | bytes 50335744 | tf_op jit(solution)/shard_map/jit(_where)/select_n | solution.py:52
  476.3 13.7 %pad_maximum_fusion.1 = bf16[2,64,64,2,256]{4,3,2,1,0:T(2,128)(2,1)} fusion(bf16[1,64,64,2,256]{4,3,2,1,0:T(2,128)(2,1)S(1)} %get-tuple-element.6, bf16[1,64,64,2,256]{4,3,2,1,0:T(2,128)(2,1)S(1)} %get-tuple-element.5), kind=kLoop, calls=%fused_computation.52 | loop fusion | flops 4194304 | bytes 16777216 | tf_op jit(solution)/shard_map/stack | solution.py:79
  490.0 13.7 %pad_maximum_fusion = bf16[2,64,64,2,256]{4,3,2,1,0:T(2,128)(2,1)} fusion(bf16[1,64,64,2,256]{4,3,2,1,0:T(2,128)(2,1)S(1)} %get-tuple-element.35, bf16[1,64,64,2,256]{4,3,2,1,0:T(2,128)(2,1)S(1)} %get-tuple-element.36), kind=kLoop, calls=%fused_computation.51 | loop fusion | flops 4194304 | bytes 16777216 | tf_op jit(solution)/shard_map/stack | solution.py:79
  503.7 42.6 %all-reduce.7.cloned.1.call-done = bf16[1024,4096]{1,0:T(8,128)(2,1)} async-done(((bf16[1024,4096]{1,0:T(8,128)(2,1)}), bf16[1024,4096]{1,0:T(8,128)(2,1)}) %all-reduce.7.cloned.1.call-update) | async-done | bytes 8388624 | tf_op jit(solution)/shard_map/psum | solution.py:77
  546.3 10.7 %fusion.9 = bf16[1024,4096]{1,0:T(8,128)(2,1)} fusion(bf16[1024,4096]{1,0:T(8,128)(2,1)} %copy-done.1, bf16[1024,4096]{1,0:T(8,128)(2,1)} %all-reduce.7.cloned.1.call-done, f32[4096]{0:T(1024)S(1)} %bitcast.163), kind=kLoop, calls=%fused_computation.12 | loop fusion | flops 20971520 | bytes 25182208 | tf_op jit(solution)/shard_map/convert_element_type | solution.py:78
  (77 shorter events, 4.1 us)
Async XLA Ops:
  7.2 272.0 %all-reduce.5.cloned.1.call-start = ((), (), s32[]{:S(2)}) async-start(), calls=%async_computation | async-start | bytes 16777216 | tf_op jit(solution)/shard_map/psum | solution.py:77
  7.2 7.1 %copy-start = (bf16[16,64,4096]{2,1,0:T(8,128)(2,1)S(1)}, bf16[16,64,4096]{2,1,0:T(8,128)(2,1)}, u32[]{:S(2)}) copy-start(bf16[16,64,4096]{2,1,0:T(8,128)(2,1)} %param.14) | copy-start | bytes 25165828
  7.3 83.8 %copy-start.23 = (pred[512]{0:T(512)(128)(4,1)}, pred[512]{0:T(512)(128)(4,1)S(1)}, u32[]{:S(2)}) copy-start(pred[512]{0:T(512)(128)(4,1)S(1)} %fusion.142) | copy-start | bytes 1540
  9.0 94.4 %copy-start.9 = (s32[64,16]{1,0:T(8,128)}, s32[64,16]{1,0:T(8,128)S(1)}, u32[]{:S(2)}) copy-start(s32[64,16]{1,0:T(8,128)S(1)} %iota_add_fusion) | copy-start | bytes 12292
  9.0 7.6 %copy-start.15 = (bf16[2,4096]{1,0:T(2,128)(2,1)S(1)}, bf16[2,4096]{1,0:T(2,128)(2,1)}, u32[]{:S(2)}) copy-start(bf16[2,4096]{1,0:T(2,128)(2,1)} %param.18) | copy-start | bytes 49156
  9.0 8.3 %copy-start.16 = (bf16[2,4096]{1,0:T(2,128)(2,1)S(1)}, bf16[2,4096]{1,0:T(2,128)(2,1)}, u32[]{:S(2)}) copy-start(bf16[2,4096]{1,0:T(2,128)(2,1)} %param.19) | copy-start | bytes 49156
  22.3 8.1 %copy-start.8 = (bf16[16,64,4096]{2,1,0:T(8,128)(2,1)}, bf16[16,64,4096]{2,1,0:T(8,128)(2,1)S(1)}, u32[]{:S(2)}) copy-start(bf16[16,64,4096]{2,1,0:T(8,128)(2,1)S(1)} %add_convert_fusion.2) | copy-start | bytes 25165828
  36.9 4.0 copy-start.3
  36.9 4.0 copy-start.21
  41.9 74.7 %copy-start.13 = (pred[64,64]{1,0:T(8,128)(4,1)}, pred[64,64]{1,0:T(8,128)(4,1)S(1)}, u32[]{:S(2)}) copy-start(pred[64,64]{1,0:T(8,128)(4,1)S(1)} %fusion.136) | copy-start | bytes 12292
  90.9 6.2 %copy-start.4 = (f32[1024,256]{0,1:T(8,128)}, f32[1024,256]{0,1:T(8,128)S(1)}, u32[]{:S(2)}) copy-start(f32[1024,256]{0,1:T(8,128)S(1)} %concatenate.35) | copy-start | bytes 3145732
  91.0 6.1 %copy-start.6 = (f32[1024,256]{0,1:T(8,128)}, f32[1024,256]{0,1:T(8,128)S(1)}, u32[]{:S(2)}) copy-start(f32[1024,256]{0,1:T(8,128)S(1)} %concatenate.32) | copy-start | bytes 3145732
  116.6 14.7 %copy-start.11 = (pred[16,64,64]{2,0,1:T(8,128)(4,1)S(1)}, pred[16,64,64]{2,0,1:T(8,128)(4,1)}, u32[]{:S(2)}) copy-start(pred[16,64,64]{2,0,1:T(8,128)(4,1)} %iota_compare_fusion) | copy-start | bytes 196612
  180.3 14.1 %copy-start.17 = (bf16[2,4096]{1,0:T(2,128)(2,1)S(1)}, bf16[2,4096]{1,0:T(2,128)(2,1)}, u32[]{:S(2)}) copy-start(bf16[2,4096]{1,0:T(2,128)(2,1)} %param.27) | copy-start | bytes 49156
  180.3 366.0 %all-reduce.7.cloned.1.call-start = ((), (), s32[]{:S(2)}) async-start(), calls=%async_computation.1 | async-start | bytes 16777216 | tf_op jit(solution)/shard_map/psum | solution.py:77
  286.8 7.0 %copy-start.1 = (bf16[1024,4096]{1,0:T(8,128)(2,1)}, bf16[1024,4096]{1,0:T(8,128)(2,1)S(1)}, u32[]{:S(2)}) copy-start(bf16[1024,4096]{1,0:T(8,128)(2,1)S(1)} %get-tuple-element.4) | copy-start | bytes 25165828
  286.8 2.4 copy-start.18
  286.8 2.4 copy-start.19
  315.3 21.5 %copy-start.10 = (s32[64,16]{1,0:T(8,128)S(1)}, s32[64,16]{1,0:T(8,128)}, u32[]{:S(2)}) copy-start(s32[64,16]{1,0:T(8,128)} %copy-done.9) | copy-start | bytes 12292
  356.6 3.3 copy-start.2
  356.6 3.3 copy-start.5
  356.6 3.4 copy-start.7
  356.6 3.4 copy-start.24
  376.1 11.0 %copy-start.14 = (pred[64,64]{1,0:T(8,128)(4,1)S(1)}, pred[64,64]{1,0:T(8,128)(4,1)}, u32[]{:S(2)}) copy-start(pred[64,64]{1,0:T(8,128)(4,1)} %copy-done.13) | copy-start | bytes 12292
  387.1 14.3 %copy-start.12 = (pred[16,64,64]{2,0,1:T(8,128)(4,1)S(1)}, pred[16,64,64]{2,0,1:T(8,128)(4,1)}, u32[]{:S(2)}) copy-start(pred[16,64,64]{2,0,1:T(8,128)(4,1)} %iota_compare_fusion) | copy-start | bytes 196612
  402.6 7.9 %copy-start.22 = (f32[1,2048]{1,0:T(1,128)S(1)}, f32[1,2048]{1,0:T(1,128)}, u32[]{:S(2)}) copy-start(f32[1,2048]{1,0:T(1,128)} %get-tuple-element.39) | copy-start | bytes 24580
  490.0 56.3 %copy-start.20 = (f32[1,4096]{1,0:T(1,128)S(1)}, f32[1,4096]{1,0:T(1,128)}, u32[]{:S(2)}) copy-start(f32[1,4096]{1,0:T(1,128)} %get-tuple-element.29) | copy-start | bytes 49156
Sparse Core Ops, SparseCore 0:
  180.4 98.6 all-reduce.4
  450.7 95.6 all-reduce.6
